TPU v7x, 256 devices: a whole 4x4x8 slice. The times are simulated.
256 devices in a mesh: tensor: 64 (over x_hi, y, z), dp: 4 (over x_lo, core).
Axes of the slice: x: 4 (x_hi: 2, x_lo: 2; x = x_hi * 2 + x_lo), y: 4, z: 8, core: 2. Of those that a mesh axis runs over, the one named last changes fastest.
Arguments:
- base_weight: bfloat16 [2, 2, 4096, 14336], P(None, None, 'tensor', 'dp'), may hold values from -0.25 to 0.25
- adapter_left: bfloat16 [2, 2, 4096, 16], P(None, None, 'tensor'), may hold values from -0.059814453 to 0.059814453
- adapter_right: bfloat16 [2, 2, 16, 14336], P(None, None, None, 'dp'), may hold values from -1.5 to 1.5
- magnitude: bfloat16 [2, 2, 14336], P(None, None, 'dp'), may hold values from 16 to 256
Outputs:
- merged_weight: bfloat16 [2, 2, 14336, 4096], P(None, None, 'tensor')
All inputs are finite; a program needn't handle non-finite values.
Results may differ from a plain program's by a relative error of at most 0.0004.
Values may be sent and summed in bfloat16 or wider, within the bound.
A program may use at most 128 MiB of HBM per device.

v0:
```python
import jax
import jax.numpy as jnp
from jax import lax
from jax.sharding import PartitionSpec as P


def cut_along(array, dim, length):
    before, after = (array.shape[:dim], array.shape[dim + 1 :])
    return jnp.moveaxis(array.reshape(*before, length, -1, *after), dim, 0)


def edges_of(length, count):
    lap = length // count
    if lap >= 8:
        lap -= lap % 8
    return [lap * k for k in range(1, count)]


def laid_out(tiles, dim):
    tiles = jnp.moveaxis(tiles, 0, dim)
    shape = tiles.shape
    return tiles.reshape(*shape[:dim], shape[dim] * shape[dim + 1], *shape[dim + 2 :])


def exchange_in_pieces(array, axis, pieces, split_dim, concat_dim):
    tiles = cut_along(array, split_dim, lax.axis_size(axis))
    split_at = max(range(1, max(2, tiles.ndim - 1)), key=lambda d: tiles.shape[d])
    finished = []
    for piece in jnp.split(tiles, edges_of(tiles.shape[split_at], pieces), axis=split_at):
        if piece.size:
            finished.append(lax.all_to_all(piece, axis, split_axis=0, concat_axis=0, tiled=True))
    return laid_out(jnp.concatenate(finished, axis=split_at), concat_dim)


def copy_for_each(array, axis):
    copies = jnp.broadcast_to(array, (lax.axis_size(axis), *array.shape))
    return lax.all_to_all(copies, axis, split_axis=0, concat_axis=0, tiled=True)


def collect(array, axis, dim):
    tiles = copy_for_each(array, axis)
    return laid_out(tiles, dim)


def turned_gather(arrays, axis, dims):
    turned = [jnp.moveaxis(a, dim, 0) for a, dim in zip(arrays, dims)]
    widths = [t[0].size for t in turned]
    both = jnp.concatenate([t.reshape(-1, w) for t, w in zip(turned, widths)], axis=1)
    whole = lax.all_gather(both, axis, axis=0, tiled=True)
    tiles = jnp.split(whole, [sum(widths[:k]) for k in range(1, len(widths))], axis=1)
    return tuple(
        (
            jnp.moveaxis(b.reshape(-1, *t.shape[1:]), 0, dim)
            for b, t, dim in zip(tiles, turned, dims)
        )
    )


def regroup(weight_slab):
    experts, projections, row_count, col_count = weight_slab.shape
    tensor_count = lax.axis_size("tensor")
    replica_count = lax.axis_size("dp")
    serve_cols = col_count * replica_count // tensor_count
    quartered = lax.all_to_all(weight_slab, "dp", split_axis=2, concat_axis=3, tiled=True)
    grouped = exchange_in_pieces(quartered, "tensor", 2, 3, 2)
    collected = lax.all_gather(grouped, "dp", axis=2, tiled=True)
    pieces_view = collected.reshape(
        experts, projections, replica_count, tensor_count, row_count // replica_count, serve_cols
    )
    return pieces_view.transpose(0, 1, 5, 3, 2, 4).reshape(
        experts, projections, serve_cols, tensor_count * row_count
    )


def shards(base_weight, adapter_left, adapter_right, magnitude):
    tensor_count = lax.axis_size("tensor")
    replica_count = lax.axis_size("dp")
    col_count = base_weight.shape[3]
    serve_cols = col_count * replica_count // tensor_count
    arrived = regroup(base_weight)
    left_full = collect(adapter_left, "tensor", 2)
    right_all, magnitude_all = turned_gather((adapter_right, magnitude), "dp", (3, 2))
    col_start = lax.axis_index("tensor") * serve_cols
    right_cols = lax.dynamic_slice_in_dim(right_all, col_start, serve_cols, 3)
    magnitude_cols = lax.dynamic_slice_in_dim(magnitude_all, col_start, serve_cols, 2)
    merged = arrived.astype(jnp.float32) + jnp.einsum(
        "xyrf,xyir->xyfi", right_cols, left_full, preferred_element_type=jnp.float32
    )
    squares = jnp.sum(merged * merged, axis=3)
    scaling = magnitude_cols.astype(jnp.float32) / jnp.sqrt(squares + 1e-06)
    return (merged * scaling[:, :, :, None]).astype(jnp.bfloat16)


def solution(mesh):
    in_specs = (
        P(None, None, "tensor", "dp"),
        P(None, None, "tensor", None),
        P(None, None, None, "dp"),
        P(None, None, "dp"),
    )
    out_specs = P(None, None, "tensor", None)
    return jax.shard_map(shards, mesh=mesh, in_specs=in_specs, out_specs=out_specs, check_vma=False)
```

profile of v0, /device:TPU:1, one launch (start us, length us, event | category | flops | bytes accessed | tf_op | source)
XLA Modules:
  0.0 277.2 jit_solution(4250908606678984291)
XLA Ops:
  6.5 3.4 %copy.9 = bf16[2,2,64,3584]{3,1,0,2:T(2,128)(2,1)S(1)} copy(bf16[2,2,64,3584]{3,2,1,0:T(8,128)(2,1)} %param.4) | data formatting | bytes 3670016 | tf_op args[0]
  9.9 27.5 %all_to_all.30 = bf16[2,2,64,3584]{3,1,0,2:T(2,128)(2,1)S(1)} all-to-all(bf16[2,2,64,3584]{3,1,0,2:T(2,128)(2,1)S(1)} %copy.9), channel_id=1, replica_groups=mesh['tensor'=64,'dp'=4] {'dp'}, dimensions={2} | all-to-all | bytes 3670016 | tf_op jit(solution)/shard_map/all_to_all | solution.py:64
  37.4 2.6 copy.18
  40.1 4.4 %reshape.29 = bf16[2,2,16,64,224]{4,3,2,1,0:T(8,128)(2,1)S(1)} reshape(bf16[2,2,16,4,3584]{4,3,2,1,0:T(4,128)(2,1)} %bitcast.45) | data formatting | bytes 3670016 | tf_op jit(solution)/shard_map/reshape | solution.py:9
  44.5 0.2 fusion.3
  44.7 1.6 copy.12
  46.2 12.6 %all-to-all-start.2 = ((bf16[64,2,2,8,224]{4,3,2,1,0:T(8,128)(2,1)}), bf16[64,2,2,8,224]{4,3,2,1,0:T(8,128)(2,1)S(1)}, u32[]{:S(2)}, u32[]{:S(2)}) async-start(bf16[64,2,2,8,224]{4,3,2,1,0:T(8,128)(2,1)} %copy.12), calls=%async_computation.2 | async-start | bytes 2097152 | tf_op jit(solution)/shard_map/all_to_all | solution.py:31
  58.8 0.0 all-gather.5.cloned.1.call-start
  58.9 0.9 pad_maximum_fusion
  59.8 0.0 all-gather.3.cloned.1.call-start
  59.8 0.6 copy.11
  60.4 26.0 %all-to-all-done.2 = bf16[64,2,2,8,224]{4,3,2,1,0:T(8,128)(2,1)S(1)} async-done(((bf16[64,2,2,8,224]{4,3,2,1,0:T(8,128)(2,1)}), bf16[64,2,2,8,224]{4,3,2,1,0:T(8,128)(2,1)S(1)}, u32[]{:S(2)}, u32[]{:S(2)}) %all-to-all-start.2) | async-done | bytes 917536 | tf_op jit(solution)/shard_map/all_to_all | solution.py:31
  86.4 34.1 %all_to_all.31 = bf16[64,2,2,8,224]{4,3,2,1,0:T(8,128)(2,1)S(1)} all-to-all(bf16[64,2,2,8,224]{4,3,2,1,0:T(8,128)(2,1)S(1)} %copy.11), channel_id=1, replica_groups=mesh['tensor'=64,'dp'=4] {'tensor'}, dimensions={0} | all-to-all | bytes 1835008 | tf_op jit(solution)/shard_map/all_to_all | solution.py:31
  120.5 0.6 maximum_bitcast_fusion
  121.1 1.5 copy.13
  122.7 0.2 broadcast_bitcast_fusion
  122.9 1.6 reshape.38
  124.5 8.6 %all-to-all-start.3 = ((bf16[64,2,2048]{2,1,0:T(2,128)(2,1)}), bf16[64,2,2048]{2,1,0:T(2,128)(2,1)S(1)}, u32[]{:S(2)}, u32[]{:S(2)}) async-start(bf16[64,2,2048]{2,1,0:T(2,128)(2,1)} %reshape.38), calls=%async_computation.3 | async-start | bytes 1048576 | tf_op jit(solution)/shard_map/all_to_all | solution.py:37
  133.1 15.9 %all-to-all-done.3 = bf16[64,2,2048]{2,1,0:T(2,128)(2,1)S(1)} async-done(((bf16[64,2,2048]{2,1,0:T(2,128)(2,1)}), bf16[64,2,2048]{2,1,0:T(2,128)(2,1)S(1)}, u32[]{:S(2)}, u32[]{:S(2)}) %all-to-all-start.3) | async-done | bytes 524320 | tf_op jit(solution)/shard_map/all_to_all | solution.py:37
  149.0 0.7 reshape.39
  149.6 0.1 bitcast_bitcast_fusion
  149.8 0.7 copy.15
  150.5 0.8 reshape.34
  151.3 1.0 split.19
  152.3 0.1 reshape.35
  152.4 57.5 %all-gather.3.cloned.1.call-done = bf16[2,2,4096,224]{3,2,1,0:T(8,128)(2,1)} async-done(((bf16[2,2,1024,224]{3,2,1,0:T(8,128)(2,1)}), bf16[2,2,4096,224]{3,2,1,0:T(8,128)(2,1)}) %all-gather.3.cloned.1.call-update) | async-done | bytes 7340048 | tf_op jit(solution)/shard_map/all_gather | solution.py:66
  209.9 11.4 %convert_bitcast_fusion = f32[2,2,224,64,4,16]{2,5,3,4,1,0:T(8,128)} fusion(bf16[2,2,4,64,16,224]{5,4,3,2,1,0:T(8,128)(2,1)} %bitcast.41), kind=kLoop, calls=%fused_computation | loop fusion | flops 3670016 | bytes 22020096 | tf_op jit(solution)/shard_map/convert_element_type | solution.py:86
  221.3 11.9 %copy.14 = f32[2,2,224,64,4,16]{2,5,4,3,1,0:T(8,128)} copy(f32[2,2,224,64,4,16]{2,5,3,4,1,0:T(8,128)} %convert_bitcast_fusion) | data formatting | bytes 29360128 | tf_op jit(solution)/shard_map/convert_element_type | solution.py:86
  233.2 17.0 %copy.16 = f32[2,2,224,4096]{3,2,1,0:T(8,128)} copy(f32[2,2,224,4096]{2,3,1,0:T(8,128)} %bitcast.40) | data formatting | bytes 29360128 | tf_op jit(solution)/shard_map/convert_element_type | solution.py:86
  250.2 9.5 %multiply_reduce_fusion = (f32[2,2,224]{2,1,0:T(2,128)S(1)}, f32[2,2,224,4096]{3,2,1,0:T(8,128)}) fusion(f32[2,2,224,4096]{3,2,1,0:T(8,128)} %copy.16, bf16[2,2,4096,16]{2,3,1,0:T(8,128)(2,1)S(1)} %reshape.34, bf16[14336,2,2,16]{0,3,2,1:T(8,128)(2,1)S(1)} %bitcast.46, s32[]{:T(128)S(6)} %select_n.4), kind=kOutput, calls=%fused_computation.2 | convolution fusion | flops 128449664 | bytes 29920772 | tf_op jit(solution)/shard_map/xyrf,xyir->xyfi/dot_general | solution.py:86
  259.7 0.1 bitcast_multiply_fusion
  259.8 10.6 %multiply_convert_fusion = bf16[2,2,224,4096]{3,2,1,0:T(8,128)(2,1)} fusion(f32[2,2,224,4096]{3,2,1,0:T(8,128)} %get-tuple-element.8, f32[2,2,224]{2,1,0:T(2,128)S(1)} %bitcast_multiply_fusion), kind=kLoop, calls=%fused_computation.1 | loop fusion | flops 7340032 | bytes 22023680 | tf_op jit(solution)/shard_map/convert_element_type | solution.py:91
  (14 shorter events, 0.1 us)
Async XLA Ops:
  6.5 116.1 %copy-start = (bf16[2,2,64,16]{2,3,1,0:T(8,128)(2,1)S(1)}, bf16[2,2,64,16]{2,3,1,0:T(8,128)(2,1)}, u32[]{:S(2)}) copy-start(bf16[2,2,64,16]{2,3,1,0:T(8,128)(2,1)} %param.5) | copy-start | bytes 24580
  44.5 14.4 %copy-start.3 = (bf16[2,2,3584]{2,1,0:T(2,128)(2,1)S(1)}, bf16[2,2,3584]{2,1,0:T(2,128)(2,1)}, u32[]{:S(2)}) copy-start(bf16[2,2,3584]{2,1,0:T(2,128)(2,1)} %param.7) | copy-start | bytes 86020
  44.7 14.2 %copy-start.2 = (bf16[2,2,16,3584]{3,2,1,0:T(8,128)(2,1)S(1)}, bf16[2,2,16,3584]{3,2,1,0:T(8,128)(2,1)}, u32[]{:S(2)}) copy-start(bf16[2,2,16,3584]{3,2,1,0:T(8,128)(2,1)} %param.6) | copy-start | bytes 1376260
  46.2 40.2 %all-to-all-start.2 = ((bf16[64,2,2,8,224]{4,3,2,1,0:T(8,128)(2,1)}), bf16[64,2,2,8,224]{4,3,2,1,0:T(8,128)(2,1)S(1)}, u32[]{:S(2)}, u32[]{:S(2)}) async-start(bf16[64,2,2,8,224]{4,3,2,1,0:T(8,128)(2,1)} %copy.12), calls=%async_computation.2 | async-start | bytes 2097152 | tf_op jit(solution)/shard_map/all_to_all | solution.py:31
  58.8 92.5 %all-gather.5.cloned.1.call-start = ((), (), s32[]{:S(2)}) async-start(), calls=%async_computation.5 | async-start | bytes 2580480 | tf_op jit(solution)/shard_map/all_gather | solution.py:49
  59.8 150.1 %all-gather.3.cloned.1.call-start = ((), (), s32[]{:S(2)}) async-start(), calls=%async_computation.4 | async-start | bytes 10485760 | tf_op jit(solution)/shard_map/all_gather | solution.py:66
  124.5 24.5 %all-to-all-start.3 = ((bf16[64,2,2048]{2,1,0:T(2,128)(2,1)}), bf16[64,2,2048]{2,1,0:T(2,128)(2,1)S(1)}, u32[]{:S(2)}, u32[]{:S(2)}) async-start(bf16[64,2,2048]{2,1,0:T(2,128)(2,1)} %reshape.38), calls=%async_computation.3 | async-start | bytes 1048576 | tf_op jit(solution)/shard_map/all_to_all | solution.py:37
  233.2 17.0 %slice-start = ((bf16[14336,68]{0,1:T(8,128)(2,1)}), bf16[14336,64]{0,1:T(8,128)(2,1)S(1)}, s32[]{:S(2)}) async-start(bf16[14336,68]{0,1:T(8,128)(2,1)} %all-gather.5.cloned.1.call-done), calls=%async_computation.6 | async-start | bytes 3670016 | tf_op jit(solution)/shard_map/split | solution.py:50
  259.8 10.6 %copy-start.1 = (bf16[2,2,64,16]{2,3,1,0:T(8,128)(2,1)S(1)}, bf16[2,2,64,16]{2,3,1,0:T(8,128)(2,1)}, u32[]{:S(2)}) copy-start(bf16[2,2,64,16]{2,3,1,0:T(8,128)(2,1)} %param.5) | copy-start | bytes 24580
Sparse Core Ops, SparseCore 0:
  61.4 38.3 all-gather.4
  122.8 87.0 all-gather.2
where the time goes:
time: 278 us; the launch traced here: 277 us
  waiting for transfers between devices  99.4 us (36%)
  blocking collectives  61.6 us (22%)
  local copies, waits for them, and re-layouts  48.4 us (17%)
  other arithmetic  23.6 us (8%)
  starting transfers between devices  21.3 us (8%)
  between operations  13.6 us (5%)
  matrix products  9.51 us (3%)
    all_gather x1, waiting for transfers between devices, regroup(): collected = lax.all_gather(grouped, 'dp', axis=2, tiled=True)  57.5 us
    all_to_all x1, blocking collectives, exchange_in_pieces(): lax.all_to_all(piece, axis, split_axis=0, concat_axis=0, tiled=True)  34.1 us
    convert_element_type x2, local copies, waits for them, and re-layouts, shards(): arrived.astype(jnp.float32)  28.9 us
    all_to_all x1, blocking collectives, regroup(): lax.all_to_all(weight_slab, 'dp', split_axis=2, concat_axis=3, tiled=True)  27.5 us
    all_to_all x1, waiting for transfers between devices, exchange_in_pieces(): lax.all_to_all(piece, axis, split_axis=0, concat_axis=0, tiled=True)  26 us
    all_to_all x1, waiting for transfers between devices, copy_for_each(): return lax.all_to_all(copies, axis, split_axis=0, concat_axis=0, tiled=True)  15.9 us
    all_to_all x1, starting transfers between devices, exchange_in_pieces(): lax.all_to_all(piece, axis, split_axis=0, concat_axis=0, tiled=True)  12.6 us
    convert_element_type x1, other arithmetic, shards(): arrived.astype(jnp.float32)  11.4 us
  transfers between devices with their start and end apart: 4, of which 3 were waited for; matrix products, arithmetic and copies ran while one was open for 3% of the time, Pallas kernels for 0%

commit v1 on v0

--- a/solution.py
+++ b/solution.py
@@ -63,7 +63,9 @@
     serve_cols = col_count * replica_count // tensor_count
     quartered = lax.all_to_all(weight_slab, "dp", split_axis=2, concat_axis=3, tiled=True)
     grouped = exchange_in_pieces(quartered, "tensor", 2, 3, 2)
-    collected = lax.all_gather(grouped, "dp", axis=2, tiled=True)
+    collected = jnp.concatenate(
+        lax.all_to_all(jnp.stack([grouped] * lax.axis_size("dp")), "dp", 0, 0), axis=2
+    )
     pieces_view = collected.reshape(
         experts, projections, replica_count, tensor_count, row_count // replica_count, serve_cols
     )

time: 278 us -> 342 us (1.23)
  waiting for transfers between devices: 99.4 us -> 155 us
  blocking collectives: 61.6 us -> 27.5 us
  local copies, waits for them, and re-layouts: 48.4 us -> 73.4 us
  starting transfers between devices: 21.3 us -> 39.8 us
    all_gather x1 -> x0, waiting for transfers between devices: 57.5 us -> none  [regroup(): collected = lax.all_gather(grouped, 'dp', axis=2, tiled=True)]
    all_to_all x0 -> x1, waiting for transfers between devices: none -> 50.7 us  [regroup(): lax.all_to_all(jnp.stack([grouped] * lax.axis_size('dp')), 'dp', 0, 0)]
    all_gather x1, waiting for transfers between devices: 0.02 us -> 40.9 us  [turned_gather(): whole = lax.all_gather(both, axis, axis=0, tiled=True)]
    all_to_all x1 -> x0, blocking collectives: 34.1 us -> none  [exchange_in_pieces(): lax.all_to_all(piece, axis, split_axis=0, concat_axis=0, tiled=True)]
    all_to_all x1 -> x2, waiting for transfers between devices: 26 us -> 50.6 us  [exchange_in_pieces(): lax.all_to_all(piece, axis, split_axis=0, concat_axis=0, tiled=True)]
    convert_element_type x2 -> x3, local copies, waits for them, and re-layouts: 28.9 us -> 44.7 us  [shards(): arrived.astype(jnp.float32)]
    all_to_all x0 -> x1, starting transfers between devices: none -> 10.5 us  [regroup(): lax.all_to_all(jnp.stack([grouped] * lax.axis_size('dp')), 'dp', 0, 0)]
    another operation x0 -> x2, local copies, waits for them, and re-layouts: none -> 7.98 us  [regroup(): jnp.stack([grouped] * lax.axis_size('dp'))]
  transfers between devices with their start and end apart: 4 -> 5, of which waited for: 3 -> 5; matrix products, arithmetic and copies ran while one was open for 3% -> 4% of each run, Pallas kernels for 0% -> 0%
where the time goes in v1:
time: 342 us; the launch traced here: 341 us
  waiting for transfers between devices  155 us (45%)
  local copies, waits for them, and re-layouts  73.4 us (21%)
  starting transfers between devices  39.8 us (12%)
  blocking collectives  27.5 us (8%)
  other arithmetic  22.3 us (7%)
  between operations  13.5 us (4%)
  matrix products  9.52 us (3%)
    all_to_all x1, waiting for transfers between devices, regroup(): lax.all_to_all(jnp.stack([grouped] * lax.axis_size('dp')), 'dp', 0, 0)  50.7 us
    all_to_all x2, waiting for transfers between devices, exchange_in_pieces(): lax.all_to_all(piece, axis, split_axis=0, concat_axis=0, tiled=True)  50.6 us
    convert_element_type x3, local copies, waits for them, and re-layouts, shards(): arrived.astype(jnp.float32)  44.7 us
    all_gather x1, waiting for transfers between devices, turned_gather(): whole = lax.all_gather(both, axis, axis=0, tiled=True)  40.9 us
    all_to_all x1, blocking collectives, regroup(): lax.all_to_all(weight_slab, 'dp', split_axis=2, concat_axis=3, tiled=True)  27.5 us
    all_to_all x2, starting transfers between devices, exchange_in_pieces(): lax.all_to_all(piece, axis, split_axis=0, concat_axis=0, tiled=True)  20.4 us
    all_to_all x1, waiting for transfers between devices, copy_for_each(): return lax.all_to_all(copies, axis, split_axis=0, concat_axis=0, tiled=True)  12.4 us
    convert_element_type x1, other arithmetic, shards(): return (merged * scaling[:, :, :, None]).astype(jnp.bfloat16)  10.6 us
  transfers between devices with their start and end apart: 5, of which 5 were waited for; matrix products, arithmetic and copies ran while one was open for 4% of the time, Pallas kernels for 0%

profile of v1, /device:TPU:1, one launch (start us, length us, event | category | flops | bytes accessed | tf_op | source)
XLA Modules:
  0.0 340.8 jit_solution(7267961644394016183)
XLA Ops:
  6.5 3.4 copy.19
  9.9 27.5 %all_to_all.35 = bf16[2,2,64,3584]{3,1,0,2:T(2,128)(2,1)S(1)} all-to-all(bf16[2,2,64,3584]{3,1,0,2:T(2,128)(2,1)S(1)} %copy.19), channel_id=1, replica_groups=mesh['tensor'=64,'dp'=4] {'dp'}, dimensions={2} | all-to-all | bytes 3670016 | tf_op jit(solution)/shard_map/all_to_all | solution.py:64
  37.4 2.6 copy.30
  40.1 4.4 %reshape.28 = bf16[2,2,16,64,224]{4,3,2,1,0:T(8,128)(2,1)S(1)} reshape(bf16[2,2,16,4,3584]{4,3,2,1,0:T(4,128)(2,1)} %bitcast.46) | data formatting | bytes 3670016 | tf_op jit(solution)/shard_map/reshape | solution.py:9
  44.6 1.6 copy.22
  46.2 12.6 %all-to-all-start.2 = ((bf16[64,2,2,8,224]{4,3,2,1,0:T(8,128)(2,1)}), bf16[64,2,2,8,224]{4,3,2,1,0:T(8,128)(2,1)S(1)}, u32[]{:S(2)}, u32[]{:S(2)}) async-start(bf16[64,2,2,8,224]{4,3,2,1,0:T(8,128)(2,1)} %copy.22), calls=%async_computation.2 | async-start | bytes 2097152 | tf_op jit(solution)/shard_map/all_to_all | solution.py:31
  58.8 1.6 copy.21
  60.4 26.0 %all-to-all-done.2 = bf16[64,2,2,8,224]{4,3,2,1,0:T(8,128)(2,1)S(1)} async-done(((bf16[64,2,2,8,224]{4,3,2,1,0:T(8,128)(2,1)}), bf16[64,2,2,8,224]{4,3,2,1,0:T(8,128)(2,1)S(1)}, u32[]{:S(2)}, u32[]{:S(2)}) %all-to-all-start.2) | async-done | bytes 917536 | tf_op jit(solution)/shard_map/all_to_all | solution.py:31
  86.4 7.8 %all-to-all-start.1 = ((bf16[64,2,2,8,224]{4,3,2,1,0:T(8,128)(2,1)}), bf16[64,2,2,8,224]{4,3,2,1,0:T(8,128)(2,1)S(1)}, u32[]{:S(2)}, u32[]{:S(2)}) async-start(bf16[64,2,2,8,224]{4,3,2,1,0:T(8,128)(2,1)} %copy.21), calls=%async_computation.1 | async-start | bytes 2097152 | tf_op jit(solution)/shard_map/all_to_all | solution.py:31
  94.2 0.2 broadcast_bitcast_fusion
  94.5 1.5 reshape.36
  96.0 24.6 %all-to-all-done.1 = bf16[64,2,2,8,224]{4,3,2,1,0:T(8,128)(2,1)S(1)} async-done(((bf16[64,2,2,8,224]{4,3,2,1,0:T(8,128)(2,1)}), bf16[64,2,2,8,224]{4,3,2,1,0:T(8,128)(2,1)S(1)}, u32[]{:S(2)}, u32[]{:S(2)}) %all-to-all-start.1) | async-done | bytes 917536 | tf_op jit(solution)/shard_map/all_to_all | solution.py:31
  120.6 8.9 %all-to-all-start.4 = ((bf16[64,2,2048]{2,1,0:T(2,128)(2,1)}), bf16[64,2,2048]{2,1,0:T(2,128)(2,1)}, u32[]{:S(2)}, u32[]{:S(2)}) async-start(bf16[64,2,2048]{2,1,0:T(2,128)(2,1)} %reshape.36), calls=%async_computation.4 | async-start | bytes 1048576 | tf_op jit(solution)/shard_map/all_to_all | solution.py:37
  129.5 0.6 maximum_bitcast_fusion
  130.2 0.2 copy.23
  130.4 2.4 copy.24
  132.8 12.4 %all-to-all-done.4 = bf16[64,2,2048]{2,1,0:T(2,128)(2,1)} async-done(((bf16[64,2,2048]{2,1,0:T(2,128)(2,1)}), bf16[64,2,2048]{2,1,0:T(2,128)(2,1)}, u32[]{:S(2)}, u32[]{:S(2)}) %all-to-all-start.4) | async-done | bytes 524320 | tf_op jit(solution)/shard_map/all_to_all | solution.py:37
  145.2 5.5 %stack.3 = bf16[4,2,2,1024,224]{3,4,2,1,0:T(8,128)(2,1)} broadcast(bf16[2,2,1024,224]{2,3,1,0:T(8,128)(2,1)} %copy.24), dimensions={1,2,3,4} | broadcast | bytes 9175040 | tf_op jit(solution)/shard_map/stack | solution.py:67
  150.8 10.5 %all-to-all-start.3 = ((bf16[4,2,2,1024,224]{3,4,2,1,0:T(8,128)(2,1)}), bf16[4,2,2,1024,224]{3,4,2,1,0:T(8,128)(2,1)}, u32[]{:S(2)}, u32[]{:S(2)}) async-start(bf16[4,2,2,1024,224]{3,4,2,1,0:T(8,128)(2,1)} %stack.3), calls=%async_computation.3 | async-start | bytes 14680064 | tf_op jit(solution)/shard_map/all_to_all | solution.py:67
  161.4 0.9 pad_maximum_fusion
  162.3 2.3 reshape.37
  164.7 0.7 copy.27
  165.4 0.8 reshape.32
  166.2 40.9 %all-gather.2.cloned.1.call-done = bf16[14336,68]{0,1:T(8,128)(2,1)} async-done(((bf16[3584,68]{0,1:T(8,128)(2,1)}), bf16[14336,68]{0,1:T(8,128)(2,1)}) %all-gather.2.cloned.1.call-update) | async-done | bytes 1949712 | tf_op jit(solution)/shard_map/all_gather | solution.py:49
  207.1 1.0 split.19
  208.2 50.7 %all-to-all-done.3 = bf16[4,2,2,1024,224]{3,4,2,1,0:T(8,128)(2,1)} async-done(((bf16[4,2,2,1024,224]{3,4,2,1,0:T(8,128)(2,1)}), bf16[4,2,2,1024,224]{3,4,2,1,0:T(8,128)(2,1)}, u32[]{:S(2)}, u32[]{:S(2)}) %all-to-all-start.3) | async-done | bytes 7340064 | tf_op jit(solution)/shard_map/all_to_all | solution.py:67
  258.9 10.2 %convert_bitcast_fusion = f32[2,2,4,1024,224]{3,4,1,0,2:T(8,128)} fusion(bf16[4,2,2,1024,224]{3,4,2,1,0:T(8,128)(2,1)} %all-to-all-done.3), kind=kLoop, calls=%fused_computation | loop fusion | flops 3670016 | bytes 22020096 | tf_op jit(solution)/shard_map/convert_element_type | solution.py:88
  269.1 15.8 %copy.25 = f32[2,2,4,1024,224]{4,3,2,1,0:T(8,128)} copy(f32[2,2,4,1024,224]{3,4,1,0,2:T(8,128)} %convert_bitcast_fusion) | data formatting | bytes 29360128 | tf_op jit(solution)/shard_map/convert_element_type | solution.py:88
  284.8 11.9 %copy.26 = f32[2,2,224,64,4,16]{2,5,4,3,1,0:T(8,128)} copy(f32[2,2,224,64,4,16]{2,5,3,4,1,0:T(8,128)} %bitcast.41) | data formatting | bytes 29360128 | tf_op jit(solution)/shard_map/convert_element_type | solution.py:88
  296.8 17.0 %copy.28 = f32[2,2,224,4096]{3,2,1,0:T(8,128)} copy(f32[2,2,224,4096]{2,3,1,0:T(8,128)} %bitcast.42) | data formatting | bytes 29360128 | tf_op jit(solution)/shard_map/convert_element_type | solution.py:88
  313.8 9.5 %multiply_reduce_fusion = (f32[2,2,224]{2,1,0:T(2,128)S(1)}, f32[2,2,224,4096]{3,2,1,0:T(8,128)}) fusion(f32[2,2,224,4096]{3,2,1,0:T(8,128)} %copy.28, bf16[2,2,4096,16]{2,3,1,0:T(8,128)(2,1)S(1)} %reshape.32, bf16[14336,2,2,16]{0,3,2,1:T(8,128)(2,1)S(1)} %bitcast.47, s32[]{:T(128)S(6)} %select_n.4), kind=kOutput, calls=%fused_computation.2 | convolution fusion | flops 128449664 | bytes 29920772 | tf_op jit(solution)/shard_map/xyrf,xyir->xyfi/dot_general | solution.py:88
  323.4 10.6 %multiply_convert_fusion = bf16[2,2,224,4096]{3,2,1,0:T(8,128)(2,1)} fusion(f32[2,2,224,4096]{3,2,1,0:T(8,128)} %get-tuple-element.8, f32[2,2,224]{2,1,0:T(2,128)S(1)} %bitcast_multiply_fusion), kind=kLoop, calls=%fused_computation.1 | loop fusion | flops 7340032 | bytes 22023680 | tf_op jit(solution)/shard_map/convert_element_type | solution.py:93
  (17 shorter events, 0.5 us)
Async XLA Ops:
  6.5 87.7 %copy-start = (bf16[2,2,64,16]{2,3,1,0:T(8,128)(2,1)S(1)}, bf16[2,2,64,16]{2,3,1,0:T(8,128)(2,1)}, u32[]{:S(2)}) copy-start(bf16[2,2,64,16]{2,3,1,0:T(8,128)(2,1)} %param.5) | copy-start | bytes 24580
  46.2 40.2 %all-to-all-start.2 = ((bf16[64,2,2,8,224]{4,3,2,1,0:T(8,128)(2,1)}), bf16[64,2,2,8,224]{4,3,2,1,0:T(8,128)(2,1)S(1)}, u32[]{:S(2)}, u32[]{:S(2)}) async-start(bf16[64,2,2,8,224]{4,3,2,1,0:T(8,128)(2,1)} %copy.22), calls=%async_computation.2 | async-start | bytes 2097152 | tf_op jit(solution)/shard_map/all_to_all | solution.py:31
  86.4 34.3 %all-to-all-start.1 = ((bf16[64,2,2,8,224]{4,3,2,1,0:T(8,128)(2,1)}), bf16[64,2,2,8,224]{4,3,2,1,0:T(8,128)(2,1)S(1)}, u32[]{:S(2)}, u32[]{:S(2)}) async-start(bf16[64,2,2,8,224]{4,3,2,1,0:T(8,128)(2,1)} %copy.21), calls=%async_computation.1 | async-start | bytes 2097152 | tf_op jit(solution)/shard_map/all_to_all | solution.py:31
  120.6 24.6 %all-to-all-start.4 = ((bf16[64,2,2048]{2,1,0:T(2,128)(2,1)}), bf16[64,2,2048]{2,1,0:T(2,128)(2,1)}, u32[]{:S(2)}, u32[]{:S(2)}) async-start(bf16[64,2,2048]{2,1,0:T(2,128)(2,1)} %reshape.36), calls=%async_computation.4 | async-start | bytes 1048576 | tf_op jit(solution)/shard_map/all_to_all | solution.py:37
  150.8 10.6 %copy-start.3 = (bf16[2,2,3584]{2,1,0:T(2,128)(2,1)S(1)}, bf16[2,2,3584]{2,1,0:T(2,128)(2,1)}, u32[]{:S(2)}) copy-start(bf16[2,2,3584]{2,1,0:T(2,128)(2,1)} %param.7) | copy-start | bytes 86020
  150.8 10.6 %copy-start.2 = (bf16[2,2,16,3584]{3,2,1,0:T(8,128)(2,1)S(1)}, bf16[2,2,16,3584]{3,2,1,0:T(8,128)(2,1)}, u32[]{:S(2)}) copy-start(bf16[2,2,16,3584]{3,2,1,0:T(8,128)(2,1)} %param.6) | copy-start | bytes 1376260
  150.8 108.1 %all-to-all-start.3 = ((bf16[4,2,2,1024,224]{3,4,2,1,0:T(8,128)(2,1)}), bf16[4,2,2,1024,224]{3,4,2,1,0:T(8,128)(2,1)}, u32[]{:S(2)}, u32[]{:S(2)}) async-start(bf16[4,2,2,1024,224]{3,4,2,1,0:T(8,128)(2,1)} %stack.3), calls=%async_computation.3 | async-start | bytes 14680064 | tf_op jit(solution)/shard_map/all_to_all | solution.py:67
  161.3 45.8 %all-gather.2.cloned.1.call-start = ((), (), s32[]{:S(2)}) async-start(), calls=%async_computation.5 | async-start | bytes 2580480 | tf_op jit(solution)/shard_map/all_gather | solution.py:49
  296.8 17.0 %slice-start = ((bf16[14336,68]{0,1:T(8,128)(2,1)}), bf16[14336,64]{0,1:T(8,128)(2,1)S(1)}, s32[]{:S(2)}) async-start(bf16[14336,68]{0,1:T(8,128)(2,1)} %all-gather.2.cloned.1.call-done), calls=%async_computation.6 | async-start | bytes 3670016 | tf_op jit(solution)/shard_map/split | solution.py:50
  323.4 10.6 %copy-start.1 = (bf16[2,2,64,16]{2,3,1,0:T(8,128)(2,1)S(1)}, bf16[2,2,64,16]{2,3,1,0:T(8,128)(2,1)}, u32[]{:S(2)}) copy-start(bf16[2,2,64,16]{2,3,1,0:T(8,128)(2,1)} %param.5) | copy-start | bytes 24580
Sparse Core Ops, SparseCore 0:
  163.9 43.1 all-gather.1
